TPU v7x, 32 devices: a whole 2x2x4 slice. The times are simulated.
32 devices in a mesh: row: 4 (over y, x), col: 8 (over z, core).
Axes of the slice: x: 2, y: 2, z: 4, core: 2. Of those that a mesh axis runs over, the one named last changes fastest.
Arguments:
- psi: bfloat16 [8192, 8192], P(('row', 'col')), may hold values from -0.125 to 0.125
- hpsi: bfloat16 [8192, 128], P(('row', 'col')), may hold values from -0.796875 to 0.796875
- slab_counts: int32 [32], P(('row', 'col')), may hold values from 1 to 256, 6144 in all
- matrix: float32 [4, 2048, 8, 1024], P('row', None, 'col'), as said below
Outputs:
- reduced: float32 [4, 2048, 8, 1024], P('row', None, 'col')
Inputs may be any that keep to these rules, and one draw needn't show every extreme that they name: Slab k's live plane waves are its first slab_counts[k] slots; the rest are padding; the counts sum to 3 * 256 * 32 // 4. The stored matrix is symmetric.
All inputs are finite; a program needn't handle non-finite values.
Results may differ from a plain program's by a relative error of at most 0.0003.
Values sent between devices are 32-bit elements; how exact they have to be, the bound alone decides.
No kernel may reach another device: no remote copies, remote signals or barrier semaphores. Data moves between devices by JAX's collectives and lax.ppermute only.
A program may use at most 64 MiB of HBM per device.

v0:
```python
import jax
import jax.numpy as jnp
from jax import lax
from jax.sharding import PartitionSpec as P

TILE = 16
HIGH = lax.Precision.HIGHEST


def lower_solve(factor, rhs):
    return lax.linalg.triangular_solve(factor, rhs, left_side=True, lower=True)


def invert_shifted(shifted):
    normal = jnp.dot(shifted.T, shifted, precision=HIGH)
    factor = jnp.linalg.cholesky(normal)
    first = lower_solve(factor, shifted.T)
    return lax.linalg.triangular_solve(factor, first, left_side=True, lower=True, transpose_a=True)


def per_device(psi, hpsi, slab_counts, matrix):
    prow_id = lax.axis_index("row")
    pcol_id = lax.axis_index("col")
    n_row = lax.axis_size("row")
    n_col = lax.axis_size("col")
    slots = psi.shape[0]
    panel = hpsi.shape[1]
    local_rows = matrix.shape[1]
    local_cols = matrix.shape[3]
    tiles_r = local_rows // TILE
    tiles_c = local_cols // TILE
    valid = jnp.arange(slots, dtype=jnp.int32) < slab_counts[0]
    hcols = jnp.where(valid[:, None], hpsi, jnp.zeros_like(hpsi))
    local_r = jnp.arange(local_rows, dtype=jnp.int32)
    local_c = jnp.arange(local_cols, dtype=jnp.int32)
    row_global = (local_r // TILE * n_row + prow_id) * TILE + local_r % TILE
    col_global = (local_c // TILE * n_col + pcol_id) * TILE + local_c % TILE
    partial_value = lax.dot_general(
        psi, hcols, (((0,), (0,)), ((), ())), preferred_element_type=jnp.float32
    )
    whole = lax.psum(partial_value, ("row", "col"))
    prow = lax.dynamic_index_in_dim(
        whole.reshape(tiles_r, n_row, TILE, panel), prow_id, 1, keepdims=False
    ).reshape(local_rows, panel)
    scols = lax.dynamic_index_in_dim(
        whole.reshape(tiles_c, n_col, TILE, panel), pcol_id, 1, keepdims=False
    ).reshape(local_cols, panel)
    span = jnp.arange(panel, dtype=jnp.int32)
    lower_r = jnp.where((row_global >= panel)[:, None], prow, jnp.zeros_like(prow))
    lower_c = jnp.where((col_global >= panel)[:, None], scols, jnp.zeros_like(scols))
    top_select = (row_global[None, :] == panel + span[:, None]).astype(jnp.float32)
    gram_part = jnp.dot(lower_r.T, lower_r, precision=HIGH)
    top_part = jnp.dot(top_select, prow, precision=HIGH)
    gram, top_rows = lax.psum((gram_part, top_part), "row")
    factor = jnp.linalg.cholesky(gram)
    basis_r = lower_solve(factor, lower_r.T).T
    basis_c = lower_solve(factor, lower_c.T).T
    top = lower_solve(factor, top_rows.T).T
    inverse = invert_shifted(jnp.eye(panel, dtype=jnp.float32) - top)
    embed_r = (row_global[:, None] == panel + span[None, :]).astype(jnp.float32)
    embed_c = (col_global[:, None] == panel + span[None, :]).astype(jnp.float32)
    reflect_r = basis_r - embed_r
    reflect_c = basis_c - embed_c
    stored = matrix[0, :, 0, :]
    col_select = (col_global[None, :] == span[:, None]).astype(jnp.float32)
    row_select = (row_global[None, :] == span[:, None]).astype(jnp.float32)
    left = jnp.dot(prow, col_select, precision=HIGH)
    upper = lax.dot_general(row_select, scols, (((0,), (1,)), ((), ())), precision=HIGH)
    inside_r = (row_global < panel)[:, None]
    inside_c = (col_global < panel)[None, :]
    refreshed = jnp.where(
        inside_r & inside_c,
        0.5 * (left + upper),
        jnp.where(inside_c, left, jnp.where(inside_r, upper, stored)),
    )
    zpart = jnp.dot(refreshed, reflect_c, precision=HIGH)
    zrows = lax.psum(zpart, "col")
    upart = lax.dot_general(refreshed, reflect_r, (((0,), (0,)), ((), ())), precision=HIGH)
    ucols = lax.psum(upart, "row")
    wmat = lax.psum(jnp.dot(reflect_r.T, zrows, precision=HIGH), "row")
    core = jnp.dot(jnp.dot(inverse, wmat, precision=HIGH), inverse.T, precision=HIGH)
    first = jnp.dot(reflect_r, jnp.dot(inverse, ucols.T, precision=HIGH), precision=HIGH)
    second = jnp.dot(
        jnp.dot(zrows, inverse.T, precision=HIGH) - jnp.dot(reflect_r, core, precision=HIGH),
        reflect_c.T,
        precision=HIGH,
    )
    return (refreshed - first - second)[None, :, None, :]


def solution(mesh):
    in_specs = (
        P(("row", "col"), None),
        P(("row", "col"), None),
        P(("row", "col")),
        P("row", None, "col", None),
    )
    out_specs = P("row", None, "col", None)
    return jax.shard_map(
        per_device, mesh=mesh, in_specs=in_specs, out_specs=out_specs, check_vma=False
    )
```

profile of v0, /device:TPU:0, one launch (start us, length us, event | category | flops | bytes accessed | tf_op | source)
XLA Modules:
  0.0 421.6 jit_solution(14257435263756658271)
XLA Ops:
  7.2 5.1 %convolution_bitcast_fusion = f32[8192,128]{0,1:T(8,128)} fusion(bf16[256,8192]{1,0:T(8,128)(2,1)} %param.7, bf16[256,128]{1,0:T(8,128)(2,1)} %param.8, pred[256]{0:T(512)(128)(4,1)S(1)} %iota_compare_fusion.9), kind=kOutput, calls=%fused_computation | convolution fusion | flops 536903680 | bytes 8454400 | tf_op jit(solution)/shard_map/dot_general | solution.py:38
  12.3 0.0 all-reduce.6.cloned.1.call-update
  12.3 0.0 all-reduce.8.cloned.1.call-start
  12.5 0.1 fusion.18
  12.6 145.3 %all-reduce.6.cloned.1.call-done = f32[8192,128]{0,1:T(8,128)} async-done(((f32[8192,128]{0,1:T(8,128)}), f32[8192,128]{0,1:T(8,128)}) %all-reduce.6.cloned.1.call-update) | async-done | bytes 4194320 | tf_op jit(solution)/shard_map/psum | solution.py:41
  157.9 5.6 %copy.11 = f32[8192,128]{1,0:T(8,128)} copy(f32[8192,128]{0,1:T(8,128)} %all-reduce.6.cloned.1.call-done) | data formatting | bytes 8388608 | tf_op jit(solution)/shard_map/psum | solution.py:41
  163.4 1.6 broadcast_select_fusion
  165.0 2.4 convolution_bitcast_fusion.1
  167.5 0.0 all-reduce.8.cloned.1.call-update
  167.5 0.0 all-reduce.10.cloned.1.call-start
  167.5 3.6 fusion.10
  171.1 1.3 broadcast_select_fusion.1
  172.4 11.0 %fusion.1 = f32[2048,1024]{1,0:T(8,128)} fusion(f32[2048,1024]{1,0:T(8,128)S(1)} %fusion.10, f32[1,2048,1,1024]{3,2,1,0:T(1,128)} %param.10, pred[1024]{0:T(1024)(128)(4,1)S(1)} %broadcast_compare_fusion.1, pred[2048]{0:T(1024)(128)(4,1)S(1)} %broadcast_compare_fusion, f32[1024,128]{1,0:T(8,128)S(1)} %bitcast.89, s32[2048]{0:T(1024)S(1)} %fusion.60), kind=kOutput, calls=%fused_computation.3 | convolution fusion | flops 3234332672 | bytes 25701376 | tf_op jit(solution)/shard_map/dot_general | solution.py:68
  183.3 1.6 fusion.4
  185.0 23.8 %all-reduce.8.cloned.1.call-done = f32[128,128]{0,1:T(8,128)} async-done(((f32[128,128]{0,1:T(8,128)}), f32[128,128]{0,1:T(8,128)}) %all-reduce.8.cloned.1.call-update) | async-done | bytes 65552 | tf_op jit(solution)/shard_map/psum | solution.py:54
  208.8 0.9 copy.16
  209.7 0.9 fusion.29
  210.5 11.7 %cholesky.44 = f32[128,128]{1,0:T(8,128)S(1)} custom-call(f32[128,128]{1,0:T(8,128)S(1)} %fusion.29), custom_call_target="Cholesky" | custom-call | tf_op jit(solution)/shard_map/jit(cholesky)/cholesky | solution.py:55
  222.3 0.7 compare_reduce_fusion.1
  223.0 0.7 fusion.12
  223.7 9.8 %custom-call.13 = f32[1,128,128]{1,2,0:T(8,128)S(1)} custom-call(f32[1,128,128]{2,1,0:T(8,128)S(1)} %fusion.12), custom_call_target="InvertDiagBlocksLowerTriangular" | custom-call | tf_op jit(solution)/shard_map/triangular_solve | solution.py:11
  233.5 0.6 convolution_subtract_fusion.2
  234.1 10.1 %fusion.77 = f32[2048,128]{1,0:T(8,128)} fusion(f32[2048,1024]{1,0:T(8,128)} %fusion.1, f32[1024,128]{1,0:T(8,128)S(1)} %convolution_subtract_fusion.2), kind=kOutput, calls=%fused_computation.122 | convolution fusion | flops 3221225472 | bytes 9961472 | tf_op jit(solution)/shard_map/dot_general | solution.py:76
  244.2 0.0 all-reduce.10.cloned.1.call-update
  244.2 0.0 all-reduce.12.cloned.1.call-start
  244.2 1.0 convolution_subtract_fusion.1
  245.2 16.6 %fusion.74 = f32[1024,128]{1,0:T(8,128)} fusion(f32[2048,1024]{1,0:T(8,128)} %fusion.1, f32[2048,128]{1,0:T(8,128)S(1)} %convolution_subtract_fusion.1), kind=kOutput, calls=%fused_computation.119 | convolution fusion | flops 3221225472 | bytes 9961472 | tf_op jit(solution)/shard_map/dot_general | solution.py:78
  261.8 41.8 %all-reduce.10.cloned.1.call-done = f32[2048,128]{1,0:T(8,128)} async-done(((f32[2048,128]{1,0:T(8,128)}), f32[2048,128]{1,0:T(8,128)}) %all-reduce.10.cloned.1.call-update) | async-done | bytes 1048592 | tf_op jit(solution)/shard_map/psum | solution.py:77
  303.7 3.7 fusion.79
  307.3 0.0 all-reduce.12.cloned.1.call-update
  307.3 46.2 %all-reduce.12.cloned.1.call-done = (f32[128,128]{1,0:T(8,128)}, f32[1024,128]{1,0:T(8,128)}, f32[128,128]{1,0:T(8,128)}) async-done(((f32[128,128]{1,0:T(8,128)}, f32[1024,128]{1,0:T(8,128)}, f32[128,128]{1,0:T(8,128)}), (f32[128,128]{1,0:T(8,128)}, f32[1024,128]{1,0:T(8,128)}, f32[128,128]{1,0:T(8,128)})) %all-reduce.12.cloned.1.call-update) | async-done | bytes 655376 | tf_op jit(solution)/shard_map/psum | solution.py:54
  353.6 1.1 fusion.25
  354.7 0.3 fusion.24
  355.0 0.1 copy.17
  355.1 11.7 %cholesky.55 = f32[128,128]{1,0:T(8,128)S(1)} custom-call(f32[128,128]{1,0:T(8,128)S(1)} %fusion.23), custom_call_target="Cholesky" | custom-call | tf_op jit(solution)/shard_map/jit(cholesky)/cholesky | solution.py:16
  366.8 0.6 compare_reduce_fusion
  367.4 0.6 fusion.13
  368.0 9.8 %custom-call.14 = f32[1,128,128]{1,2,0:T(8,128)S(1)} custom-call(f32[1,128,128]{2,1,0:T(8,128)S(1)} %fusion.13), custom_call_target="InvertDiagBlocksLowerTriangular" | custom-call | tf_op jit(solution)/shard_map/triangular_solve | solution.py:18
  377.8 0.3 fusion.19
  378.1 0.2 fusion.21
  378.3 1.0 fusion.80
  379.4 0.3 fusion.81
  379.7 1.8 fusion.75
  381.4 7.2 %fusion.76 = f32[2048,1024]{1,0:T(8,128)S(1)} fusion(f32[2048,128]{1,0:T(8,128)S(1)} %convolution_subtract_fusion.1, f32[128,1024]{1,0:T(8,128)S(1)} %fusion.75), kind=kOutput, calls=%fused_computation.121 | convolution fusion | flops 3221225472 | bytes 9961472 | tf_op jit(solution)/shard_map/dot_general | solution.py:82
  388.7 1.0 fusion.78
  389.7 1.0 convolution_subtract_fusion
  390.7 8.0 %subtract_bitcast_fusion = f32[1,2048,1,1024]{3,1,2,0:T(8,128)S(1)} fusion(f32[2048,1024]{1,0:T(8,128)S(1)} %bitcast.83, f32[2048,1024]{1,0:T(8,128)S(1)} %fusion.76, f32[2048,128]{1,0:T(8,128)S(1)} %convolution_subtract_fusion, f32[1024,128]{1,0:T(8,128)S(1)} %convolution_subtract_fusion.2), kind=kOutput, calls=%fused_computation.4 | convolution fusion | flops 3225419776 | bytes 26738688 | tf_op jit(solution)/shard_map/dot_general | solution.py:83
  398.7 16.1 %copy.18 = f32[1,2048,1,1024]{3,2,1,0:T(1,128)} copy(f32[1,2048,1,1024]{3,1,2,0:T(8,128)S(1)} %subtract_bitcast_fusion) | data formatting | bytes 16777216 | tf_op jit(solution)/shard_map/broadcast_in_dim | solution.py:88
  (18 shorter events, 0.2 us)
Async XLA Ops:
  6.5 151.3 %all-reduce.6.cloned.1.call-start = ((), (), s32[]{:S(2)}) async-start(), calls=%async_computation | async-start | bytes 8388608 | tf_op jit(solution)/shard_map/psum | solution.py:41
  12.3 196.4 %all-reduce.8.cloned.1.call-start = ((), (), s32[]{:S(2)}) async-start(), calls=%async_computation.1 | async-start | bytes 131072 | tf_op jit(solution)/shard_map/psum | solution.py:54
  167.5 136.2 %all-reduce.10.cloned.1.call-start = ((), (), s32[]{:S(2)}) async-start(), calls=%async_computation.2 | async-start | bytes 2097152 | tf_op jit(solution)/shard_map/psum | solution.py:77
  244.2 109.4 %all-reduce.12.cloned.1.call-start = ((), (), s32[]{:S(2)}) async-start(), calls=%async_computation.3 | async-start | bytes 1310720 | tf_op jit(solution)/shard_map/psum | solution.py:54
  379.6 9.0 %copy-start = (f32[2048,128]{1,0:T(8,128)S(1)}, f32[2048,128]{1,0:T(8,128)}, u32[]{:S(2)}) copy-start(f32[2048,128]{1,0:T(8,128)} %all-reduce.10.cloned.1.call-done) | copy-start | bytes 3145732
  379.6 11.0 %slice-start = ((s8[8388608]{0:T(1024)(128)(4,1)}), s8[4194304]{0:T(1024)(128)(4,1)S(1)}, s32[]{:S(2)}) async-start(s8[8388608]{0:T(1024)(128)(4,1)} %bitcast.82), calls=%async_computation.4 | async-start | bytes 8388608
  381.4 9.3 %slice-start.1 = ((s8[8388608]{0:T(1024)(128)(4,1)}), s8[4194304]{0:T(1024)(128)(4,1)S(1)}, s32[]{:S(2)}) async-start(s8[8388608]{0:T(1024)(128)(4,1)} %bitcast.82), calls=%async_computation.5 | async-start | bytes 8388608
Sparse Core Ops, SparseCore 0:
  12.9 144.9 all-reduce.5
  167.6 41.1 all-reduce.7
  244.3 59.2 all-reduce.9
  307.5 46.0 all-reduce.11
where the time goes:
time: 428 us; the launch traced here: 422 us
  waiting for transfers between devices  257 us (60%)
  matrix products  77.7 us (18%)
  other arithmetic  49.6 us (12%)
  local copies, waits for them, and re-layouts  22.7 us (5%)
  between operations  14.3 us (3%)
    psum x1, waiting for transfers between devices, per_device(): whole = lax.psum(partial_value, ('row', 'col'))  145 us
    psum x2, waiting for transfers between devices, per_device(): gram, top_rows = lax.psum((gram_part, top_part), 'row')  70 us
    psum x1, waiting for transfers between devices, per_device(): zrows = lax.psum(zpart, 'col')  41.8 us
    dot_general x1, matrix products, per_device(): lax.dot_general(refreshed, reflect_r, (((0,), (0,)), ((), ())), precision...  16.6 us
    broadcast_in_dim x1, local copies, waits for them, and re-layouts, per_device(): return (refreshed - first - second)[None, :, None, :]  16.1 us
    another operation x3, other arithmetic, per_device(): factor = jnp.linalg.cholesky(gram)  12.5 us
    another operation x3, other arithmetic, invert_shifted(): factor = jnp.linalg.cholesky(normal)  12.4 us
    dot_general x1, matrix products, per_device(): lax.dot_general(row_select, scols, (((0,), (1,)), ((), ())), precision=HIGH)  11 us
  transfers between devices with their start and end apart: 4, of which 4 were waited for; matrix products, arithmetic and copies ran while one was open for 8% of the time, Pallas kernels for 0%

commit v1 on v0

--- a/solution.py
+++ b/solution.py
@@ -74,7 +74,7 @@
         jnp.where(inside_c, left, jnp.where(inside_r, upper, stored)),
     )
     zpart = jnp.dot(refreshed, reflect_c, precision=HIGH)
-    zrows = lax.psum(zpart, "col")
+    zrows = jnp.sum(lax.all_gather(zpart, "col"), axis=0)
     upart = lax.dot_general(refreshed, reflect_r, (((0,), (0,)), ((), ())), precision=HIGH)
     ucols = lax.psum(upart, "row")
     wmat = lax.psum(jnp.dot(reflect_r.T, zrows, precision=HIGH), "row")

time: 428 us -> 453 us (1.058)
  waiting for transfers between devices: 257 us -> 279 us
    all_gather x0 -> x1, waiting for transfers between devices: none -> 62.8 us  [per_device(): zrows = jnp.sum(lax.all_gather(zpart, 'col'), axis=0)]
    psum x1 -> x0, waiting for transfers between devices: 41.8 us -> none  [per_device(): zrows = lax.psum(zpart, 'col')]
where the time goes in v1:
time: 453 us; the launch traced here: 446 us
  waiting for transfers between devices  279 us (62%)
  matrix products  76.6 us (17%)
  other arithmetic  53.5 us (12%)
  local copies, waits for them, and re-layouts  22.7 us (5%)
  between operations  14.3 us (3%)
    psum x1, waiting for transfers between devices, per_device(): whole = lax.psum(partial_value, ('row', 'col'))  145 us
    psum x2, waiting for transfers between devices, per_device(): gram, top_rows = lax.psum((gram_part, top_part), 'row')  71.1 us
    all_gather x1, waiting for transfers between devices, per_device(): zrows = jnp.sum(lax.all_gather(zpart, 'col'), axis=0)  62.8 us
    dot_general x1, matrix products, per_device(): lax.dot_general(refreshed, reflect_r, (((0,), (0,)), ((), ())), precision...  16.7 us
    broadcast_in_dim x1, local copies, waits for them, and re-layouts, per_device(): return (refreshed - first - second)[None, :, None, :]  16.1 us
    another operation x3, other arithmetic, per_device(): factor = jnp.linalg.cholesky(gram)  12.5 us
    another operation x3, other arithmetic, invert_shifted(): factor = jnp.linalg.cholesky(normal)  12.4 us
    dot_general x1, matrix products, per_device(): lax.dot_general(row_select, scols, (((0,), (1,)), ((), ())), precision=HIGH)  11 us
  transfers between devices with their start and end apart: 4, of which 4 were waited for; matrix products, arithmetic and copies ran while one was open for 8% of the time, Pallas kernels for 0%

profile of v1, /device:TPU:0, one launch (start us, length us, event | category | flops | bytes accessed | tf_op | source)
XLA Modules:
  0.0 446.5 jit_solution(15138276162760494329)
XLA Ops:
  7.2 5.1 %convolution_bitcast_fusion = f32[8192,128]{0,1:T(8,128)} fusion(bf16[256,8192]{1,0:T(8,128)(2,1)} %param.7, bf16[256,128]{1,0:T(8,128)(2,1)} %param.8, pred[256]{0:T(512)(128)(4,1)S(1)} %iota_compare_fusion.9), kind=kOutput, calls=%fused_computation | convolution fusion | flops 536903680 | bytes 8454400 | tf_op jit(solution)/shard_map/dot_general | solution.py:38
  12.3 0.0 all-reduce.5.cloned.1.call-update
  12.3 0.0 all-reduce.7.cloned.1.call-start
  12.5 0.1 fusion.18
  12.6 145.3 %all-reduce.5.cloned.1.call-done = f32[8192,128]{0,1:T(8,128)} async-done(((f32[8192,128]{0,1:T(8,128)}), f32[8192,128]{0,1:T(8,128)}) %all-reduce.5.cloned.1.call-update) | async-done | bytes 4194320 | tf_op jit(solution)/shard_map/psum | solution.py:41
  157.9 5.6 %copy.11 = f32[8192,128]{1,0:T(8,128)} copy(f32[8192,128]{0,1:T(8,128)} %all-reduce.5.cloned.1.call-done) | data formatting | bytes 8388608 | tf_op jit(solution)/shard_map/psum | solution.py:41
  163.4 1.6 broadcast_select_fusion
  165.0 2.4 convolution_bitcast_fusion.1
  167.5 0.0 all-gather.3.cloned.1.call-start
  167.5 3.6 fusion.10
  171.1 1.3 broadcast_select_fusion.1
  172.4 11.0 %fusion.1 = f32[2048,1024]{1,0:T(8,128)} fusion(f32[2048,1024]{1,0:T(8,128)S(1)} %fusion.10, f32[1,2048,1,1024]{3,2,1,0:T(1,128)} %param.10, pred[1024]{0:T(1024)(128)(4,1)S(1)} %broadcast_compare_fusion.1, pred[2048]{0:T(1024)(128)(4,1)S(1)} %broadcast_compare_fusion, f32[1024,128]{1,0:T(8,128)S(1)} %bitcast.91, s32[2048]{0:T(1024)S(1)} %fusion.60), kind=kOutput, calls=%fused_computation.3 | convolution fusion | flops 3234332672 | bytes 25701376 | tf_op jit(solution)/shard_map/dot_general | solution.py:68
  183.3 25.4 %all-reduce.7.cloned.1.call-done = f32[128,128]{0,1:T(8,128)} async-done(((f32[128,128]{0,1:T(8,128)}), f32[128,128]{0,1:T(8,128)}) %all-reduce.7.cloned.1.call-update) | async-done | bytes 65552 | tf_op jit(solution)/shard_map/psum | solution.py:54
  208.8 0.9 copy.16
  209.7 0.9 fusion.29
  210.5 11.7 %cholesky.44 = f32[128,128]{1,0:T(8,128)S(1)} custom-call(f32[128,128]{1,0:T(8,128)S(1)} %fusion.29), custom_call_target="Cholesky" | custom-call | tf_op jit(solution)/shard_map/jit(cholesky)/cholesky | solution.py:55
  222.3 0.7 compare_reduce_fusion.1
  223.0 0.7 fusion.12
  223.7 9.8 %custom-call.13 = f32[1,128,128]{1,2,0:T(8,128)S(1)} custom-call(f32[1,128,128]{2,1,0:T(8,128)S(1)} %fusion.12), custom_call_target="InvertDiagBlocksLowerTriangular" | custom-call | tf_op jit(solution)/shard_map/triangular_solve | solution.py:11
  233.5 0.6 convolution_subtract_fusion.2
  234.1 10.1 %fusion.77 = f32[2048,128]{1,0:T(8,128)} fusion(f32[2048,1024]{1,0:T(8,128)} %fusion.1, f32[1024,128]{1,0:T(8,128)S(1)} %convolution_subtract_fusion.2), kind=kOutput, calls=%fused_computation.122 | convolution fusion | flops 3221225472 | bytes 9961472 | tf_op jit(solution)/shard_map/dot_general | solution.py:76
  244.2 0.0 all-gather.3.cloned.1.call-update
  244.3 0.0 all-reduce.9.cloned.1.call-start
  244.3 1.7 fusion.4
  246.0 1.0 convolution_subtract_fusion.1
  246.9 16.7 %fusion.74 = f32[1024,128]{1,0:T(8,128)} fusion(f32[2048,1024]{1,0:T(8,128)} %fusion.1, f32[2048,128]{1,0:T(8,128)S(1)} %convolution_subtract_fusion.1), kind=kOutput, calls=%fused_computation.119 | convolution fusion | flops 3221225472 | bytes 9961472 | tf_op jit(solution)/shard_map/dot_general | solution.py:78
  263.6 62.8 %all-gather.3.cloned.1.call-done = f32[16384,128]{1,0:T(8,128)} async-done(((f32[2048,128]{1,0:T(8,128)}), f32[16384,128]{1,0:T(8,128)}) %all-gather.3.cloned.1.call-update) | async-done | bytes 8388624 | tf_op jit(solution)/shard_map/all_gather | solution.py:77
  326.4 3.9 reduce_sum.9
  330.3 2.4 fusion.79
  332.8 0.0 all-reduce.9.cloned.1.call-update
  332.8 45.6 %all-reduce.9.cloned.1.call-done = (f32[128,128]{1,0:T(8,128)}, f32[1024,128]{1,0:T(8,128)}, f32[128,128]{1,0:T(8,128)}) async-done(((f32[128,128]{1,0:T(8,128)}, f32[1024,128]{1,0:T(8,128)}, f32[128,128]{1,0:T(8,128)}), (f32[128,128]{1,0:T(8,128)}, f32[1024,128]{1,0:T(8,128)}, f32[128,128]{1,0:T(8,128)})) %all-reduce.9.cloned.1.call-update) | async-done | bytes 655376 | tf_op jit(solution)/shard_map/psum | solution.py:54
  378.5 1.1 fusion.25
  379.6 0.3 fusion.24
  379.9 0.1 copy.17
  380.0 11.7 %cholesky.55 = f32[128,128]{1,0:T(8,128)S(1)} custom-call(f32[128,128]{1,0:T(8,128)S(1)} %fusion.23), custom_call_target="Cholesky" | custom-call | tf_op jit(solution)/shard_map/jit(cholesky)/cholesky | solution.py:16
  391.7 0.6 compare_reduce_fusion
  392.4 0.6 fusion.13
  392.9 9.8 %custom-call.14 = f32[1,128,128]{1,2,0:T(8,128)S(1)} custom-call(f32[1,128,128]{2,1,0:T(8,128)S(1)} %fusion.13), custom_call_target="InvertDiagBlocksLowerTriangular" | custom-call | tf_op jit(solution)/shard_map/triangular_solve | solution.py:18
  402.7 0.3 fusion.19
  403.0 0.2 fusion.21
  403.2 1.0 fusion.78
  404.3 1.0 fusion.80
  405.3 0.3 fusion.81
  405.6 1.8 fusion.75
  407.4 7.2 %fusion.76 = f32[2048,1024]{1,0:T(8,128)S(1)} fusion(f32[2048,128]{1,0:T(8,128)S(1)} %convolution_subtract_fusion.1, f32[128,1024]{1,0:T(8,128)S(1)} %fusion.75), kind=kOutput, calls=%fused_computation.121 | convolution fusion | flops 3221225472 | bytes 9961472 | tf_op jit(solution)/shard_map/dot_general | solution.py:82
  414.6 1.0 convolution_subtract_fusion
  415.6 8.0 %subtract_bitcast_fusion = f32[1,2048,1,1024]{3,1,2,0:T(8,128)S(1)} fusion(f32[2048,1024]{1,0:T(8,128)S(1)} %bitcast.84, f32[2048,1024]{1,0:T(8,128)S(1)} %fusion.76, f32[2048,128]{1,0:T(8,128)S(1)} %convolution_subtract_fusion, f32[1024,128]{1,0:T(8,128)S(1)} %convolution_subtract_fusion.2), kind=kOutput, calls=%fused_computation.4 | convolution fusion | flops 3225419776 | bytes 26738688 | tf_op jit(solution)/shard_map/dot_general | solution.py:83
  423.6 16.1 %copy.18 = f32[1,2048,1,1024]{3,2,1,0:T(1,128)} copy(f32[1,2048,1,1024]{3,1,2,0:T(8,128)S(1)} %subtract_bitcast_fusion) | data formatting | bytes 16777216 | tf_op jit(solution)/shard_map/broadcast_in_dim | solution.py:88
  (17 shorter events, 0.2 us)
Async XLA Ops:
  6.5 151.3 %all-reduce.5.cloned.1.call-start = ((), (), s32[]{:S(2)}) async-start(), calls=%async_computation | async-start | bytes 8388608 | tf_op jit(solution)/shard_map/psum | solution.py:41
  12.3 196.4 %all-reduce.7.cloned.1.call-start = ((), (), s32[]{:S(2)}) async-start(), calls=%async_computation.1 | async-start | bytes 131072 | tf_op jit(solution)/shard_map/psum | solution.py:54
  167.5 159.0 %all-gather.3.cloned.1.call-start = ((), (), s32[]{:S(2)}) async-start(), calls=%async_computation.2 | async-start | bytes 9437184 | tf_op jit(solution)/shard_map/all_gather | solution.py:77
  244.3 134.2 %all-reduce.9.cloned.1.call-start = ((), (), s32[]{:S(2)}) async-start(), calls=%async_computation.3 | async-start | bytes 1310720 | tf_op jit(solution)/shard_map/psum | solution.py:54
  405.6 10.0 %slice-start = ((s8[8388608]{0:T(1024)(128)(4,1)}), s8[4194304]{0:T(1024)(128)(4,1)S(1)}, s32[]{:S(2)}) async-start(s8[8388608]{0:T(1024)(128)(4,1)} %bitcast.83), calls=%async_computation.4 | async-start | bytes 8388608
  407.4 8.2 %slice-start.1 = ((s8[8388608]{0:T(1024)(128)(4,1)}), s8[4194304]{0:T(1024)(128)(4,1)S(1)}, s32[]{:S(2)}) async-start(s8[8388608]{0:T(1024)(128)(4,1)} %bitcast.83), calls=%async_computation.5 | async-start | bytes 8388608
Sparse Core Ops, SparseCore 0:
  12.9 144.9 all-reduce.4
  167.6 41.1 all-reduce.6
  244.4 82.0 all-gather.2
  332.9 45.4 all-reduce.8
